TPU v7x, 256 devices: a whole 4x4x8 slice. The times are simulated.
256 devices in a mesh: row: 16 (over z, core), col: 16 (over x, y).
Axes of the slice: x: 4, y: 4, z: 8, core: 2. Of those that a mesh axis runs over, the one named last changes fastest.
Arguments:
- hamiltonian: bfloat16 [36864, 36864], P('row', 'col'), may hold values from -0.6 to 0.6, as said below
- start_vectors: float32 [8, 16, 2304], P(None, 'col', 'row'), may hold values from -20 to 20
Outputs:
- last_vectors: float32 [8, 36864], P(None, ('row', 'col'))
- moments: float32 [8, 4], replicated
Inputs may be any that keep to these rules, and one draw needn't show every extreme that they name: `hamiltonian`: the matrix is exactly symmetric.
All inputs are finite; a program needn't handle non-finite values.
Results may differ from a plain program's by a relative error of at most 0.0024.
Values may be sent and summed in bfloat16 or wider, within the bound.
A program may use at most 64 MiB of HBM per device.

v0:
```python
import functools

import jax
import jax.numpy as jnp
from jax import lax
from jax.sharding import Mesh
from jax.sharding import PartitionSpec as P

STEPS = 3
ORDER = 36864
COL = ("col_0", "col_1")
ROW = ("row_0", "row_1")
ROW_COL = ("row_0", "row_1", "col_0", "col_1")


def in_blocks(value, dim, size):
    shape = value.shape
    pieces = value.reshape(*shape[:dim], size, shape[dim] // size, *shape[dim + 1 :])
    return jnp.moveaxis(pieces, dim, 0)


def summed_on_arrival(value, axis, dim):
    pieces = in_blocks(value, dim, lax.axis_size(axis))
    arrived = lax.all_to_all(pieces, axis, split_axis=0, concat_axis=0, tiled=True)
    return arrived.sum(axis=0)


def sent_to_all(value, axis):
    size = lax.axis_size(axis)
    return lax.all_to_all(
        jnp.broadcast_to(value[None], (size, *value.shape)), axis, 0, 0, tiled=True
    )


def laid_out(pieces, dim):
    pieces = jnp.moveaxis(pieces, 0, dim)
    shape = pieces.shape
    return pieces.reshape(*shape[:dim], shape[dim] * shape[dim + 1], *shape[dim + 2 :])


def gather_directly(value, axis, dim):
    pieces = sent_to_all(value, axis)
    return laid_out(pieces, dim)


def over_axes(value, axes):
    return functools.reduce(lax.psum, axes, value)


def reduce_cols(product):
    return summed_on_arrival(product, COL, 1)


def reduce_rows(product):
    return summed_on_arrival(product, ROW, 1)


def from_columns(narrow, hamiltonian):
    vec_count = narrow.shape[0]

    def accumulate(running, portion, offset):
        return lax.dot_general(
            portion, hamiltonian, (((1,), (1,)), ((), ())), preferred_element_type=jnp.float32
        )

    empty = jnp.zeros((vec_count, hamiltonian.shape[0]), jnp.float32)
    return accumulate(empty, gather_directly(narrow, ROW, 1), jnp.int32(0))


def from_rows(narrow, hamiltonian):
    vec_count = narrow.shape[0]

    def accumulate(running, portion, offset):
        return jnp.dot(portion, hamiltonian, preferred_element_type=jnp.float32)

    empty = jnp.zeros((vec_count, hamiltonian.shape[1]), jnp.float32)
    return accumulate(empty, gather_directly(narrow, COL, 1), jnp.int32(0))


def per_device(hamiltonian, start_vectors):
    current = start_vectors[:, 0, :]
    partials = [jnp.sum(current * current, axis=1) / ORDER]
    previous = current
    for level in range(STEPS):
        narrow = current.astype(jnp.bfloat16)
        if level % 2 == 0:
            applied = reduce_cols(from_columns(narrow, hamiltonian))
        else:
            applied = reduce_rows(from_rows(narrow, hamiltonian))
        if level == 0:
            following = applied
        else:
            following = 2.0 * applied - previous
        previous = current
        current = following
        partials.append(jnp.sum(current * current, axis=1) / ORDER)
    squares = over_axes(jnp.stack(partials, axis=1), ROW_COL)
    moments = jnp.concatenate([squares[:, :1], 2.0 * squares[:, 1:] - squares[:, :1]], axis=1)
    return (current, moments)


def solution(mesh):
    finer = Mesh(mesh.devices.reshape(8, 2, 4, 4), ("row_0", "row_1", "col_0", "col_1"))
    return jax.shard_map(
        per_device,
        mesh=finer,
        in_specs=(P(ROW, COL), P(None, COL, ROW)),
        out_specs=(P(None, ROW_COL), P()),
        check_vma=False,
    )
```

profile of v0, /device:TPU:2, one launch (start us, length us, event | category | flops | bytes accessed | tf_op | source)
XLA Modules:
  0.0 143.0 jit_solution(12970105808916233958)
XLA Ops:
  0.6 0.7 copy.18
  1.3 16.1 %all_to_all.30 = bf16[16,8,144]{2,1,0:T(8,128)(2,1)S(1)} all-to-all(bf16[16,8,144]{2,1,0:T(8,128)(2,1)S(1)} %broadcast_in_dim.6), channel_id=1, replica_groups=mesh['row_0'=8,'row_1'=2,'col_0'=4,'col_1'=4] {'row_0','row_1'}, dimensions={0} | all-to-all | bytes 73728 | tf_op jit(solution)/shard_map/all_to_all | solution.py:30
  17.5 0.1 reshape.75
  17.6 5.5 %convolution_bitcast_fusion.2 = f32[16,8,144]{2,1,0:T(8,128)S(1)} fusion(bf16[8,2304,1]{1,0,2:T(8,128)(2,1)S(1)} %reshape.75, bf16[16,144,2304]{2,1,0:T(8,128)(2,1)} %bitcast.40), kind=kOutput, calls=%fused_computation.2 | convolution fusion | flops 84934656 | bytes 10727424 | tf_op jit(solution)/shard_map/dot_general | solution.py:62
  23.2 13.7 %all_to_all.31 = f32[16,8,144]{2,1,0:T(8,128)S(1)} all-to-all(f32[16,8,144]{2,1,0:T(8,128)S(1)} %convolution_bitcast_fusion.2), channel_id=1, replica_groups=mesh['row_0'=8,'row_1'=2,'col_0'=4,'col_1'=4] {'col_0','col_1'}, dimensions={0} | all-to-all | bytes 147456 | tf_op jit(solution)/shard_map/all_to_all | solution.py:24
  36.9 0.6 broadcast_in_dim.7
  37.5 5.1 %all-to-all-start.2 = ((bf16[16,8,144]{2,1,0:T(8,128)(2,1)}), bf16[16,8,144]{2,1,0:T(8,128)(2,1)S(1)}, u32[]{:S(2)}, u32[]{:S(2)}) async-start(bf16[16,8,144]{2,1,0:T(8,128)(2,1)} %broadcast_in_dim.7), calls=%async_computation.2 | async-start | bytes 131072 | tf_op jit(solution)/shard_map/all_to_all | solution.py:30
  42.6 14.4 %copy.8 = bf16[2304,2304]{0,1:T(8,128)(2,1)} copy(bf16[2304,2304]{1,0:T(8,128)(2,1)} %param.2) | data formatting | bytes 21233664 | tf_op args[0]
  57.0 0.0 all-to-all-done.2
  57.1 0.1 reshape.76
  57.2 5.5 %convolution_bitcast_fusion.1 = f32[16,8,144]{2,1,0:T(8,128)S(1)} fusion(bf16[8,2304,1]{1,0,2:T(8,128)(2,1)S(1)} %reshape.76, bf16[16,144,2304]{2,1,0:T(8,128)(2,1)} %bitcast.42), kind=kOutput, calls=%fused_computation.1 | convolution fusion | flops 84934656 | bytes 10727424 | tf_op jit(solution)/shard_map/dot_general | solution.py:74
  62.8 11.3 %all_to_all.32 = f32[16,8,144]{2,1,0:T(8,128)S(1)} all-to-all(f32[16,8,144]{2,1,0:T(8,128)S(1)} %convolution_bitcast_fusion.1), channel_id=1, replica_groups=mesh['row_0'=8,'row_1'=2,'col_0'=4,'col_1'=4] {'row_0','row_1'}, dimensions={0} | all-to-all | bytes 147456 | tf_op jit(solution)/shard_map/all_to_all | solution.py:24
  74.0 0.1 fusion
  74.2 10.7 %all_to_all.33 = bf16[16,8,144]{2,1,0:T(8,128)(2,1)S(1)} all-to-all(bf16[16,8,144]{2,1,0:T(8,128)(2,1)S(1)} %broadcast_in_dim.8), channel_id=1, replica_groups=mesh['row_0'=8,'row_1'=2,'col_0'=4,'col_1'=4] {'row_0','row_1'}, dimensions={0} | all-to-all | bytes 73728 | tf_op jit(solution)/shard_map/all_to_all | solution.py:30
  84.9 0.1 reshape.77
  85.0 7.5 %convolution_bitcast_fusion = f32[16,8,144]{2,1,0:T(8,128)} fusion(bf16[8,2304,1]{1,0,2:T(8,128)(2,1)S(1)} %reshape.77, bf16[16,144,2304]{2,1,0:T(8,128)(2,1)} %bitcast.41), kind=kOutput, calls=%fused_computation | convolution fusion | flops 84934656 | bytes 10727424 | tf_op jit(solution)/shard_map/dot_general | solution.py:62
  92.5 7.2 %all-to-all-start.5 = ((f32[16,8,144]{2,1,0:T(8,128)}), f32[16,8,144]{2,1,0:T(8,128)S(1)}, u32[]{:S(2)}, u32[]{:S(2)}) async-start(f32[16,8,144]{2,1,0:T(8,128)} %convolution_bitcast_fusion), calls=%async_computation.5 | async-start | bytes 262144 | tf_op jit(solution)/shard_map/all_to_all | solution.py:24
  99.8 6.4 %all-to-all-done.5 = f32[16,8,144]{2,1,0:T(8,128)S(1)} async-done(((f32[16,8,144]{2,1,0:T(8,128)}), f32[16,8,144]{2,1,0:T(8,128)S(1)}, u32[]{:S(2)}, u32[]{:S(2)}) %all-to-all-start.5) | async-done | bytes 73760 | tf_op jit(solution)/shard_map/all_to_all | solution.py:24
  106.2 0.7 multiply_reduce_fusion
  106.9 14.8 %psum.28 = f32[8,4]{0,1:T(4,128)S(1)} all-reduce(f32[8,4]{0,1:T(4,128)S(1)} %pad_maximum_fusion), channel_id=1, replica_groups=mesh['row_0'=8,'row_1'=2,'col_0'=4,'col_1'=4] {'row_0'}, use_global_device_ids=true, to_apply=%region_7.0 | all-reduce | flops 32 | bytes 256 | tf_op jit(solution)/shard_map/psum | solution.py:47
  121.7 2.5 %psum.29 = f32[8,4]{0,1:T(4,128)S(1)} all-reduce(f32[8,4]{0,1:T(4,128)S(1)} %psum.28), channel_id=1, replica_groups=mesh['row_0'=8,'row_1'=2,'col_0'=4,'col_1'=4] {'row_1'}, use_global_device_ids=true, to_apply=%region_8.0 | all-reduce | flops 32 | bytes 256 | tf_op jit(solution)/shard_map/psum | solution.py:47
  124.2 9.2 %psum.30 = f32[8,4]{0,1:T(4,128)S(1)} all-reduce(f32[8,4]{0,1:T(4,128)S(1)} %psum.29), channel_id=1, replica_groups=mesh['row_0'=8,'row_1'=2,'col_0'=4,'col_1'=4] {'col_0'}, use_global_device_ids=true, to_apply=%region_9.0 | all-reduce | flops 32 | bytes 256 | tf_op jit(solution)/shard_map/psum | solution.py:47
  133.4 9.0 %psum.31 = f32[8,4]{0,1:T(4,128)S(1)} all-reduce(f32[8,4]{0,1:T(4,128)S(1)} %psum.30), channel_id=1, replica_groups=mesh['row_0'=8,'row_1'=2,'col_0'=4,'col_1'=4] {'col_1'}, use_global_device_ids=true, to_apply=%region_10.0 | all-reduce | flops 32 | bytes 256 | tf_op jit(solution)/shard_map/psum | solution.py:47
  142.4 0.6 pad_maximum_fusion.1
  (16 shorter events, 0.2 us)
Async XLA Ops:
  37.5 19.5 %all-to-all-start.2 = ((bf16[16,8,144]{2,1,0:T(8,128)(2,1)}), bf16[16,8,144]{2,1,0:T(8,128)(2,1)S(1)}, u32[]{:S(2)}, u32[]{:S(2)}) async-start(bf16[16,8,144]{2,1,0:T(8,128)(2,1)} %broadcast_in_dim.7), calls=%async_computation.2 | async-start | bytes 131072 | tf_op jit(solution)/shard_map/all_to_all | solution.py:30
  57.0 17.0 %copy-start = (f32[8,1,144]{2,1,0:T(1,128)S(1)}, f32[8,1,144]{2,1,0:T(1,128)}, u32[]{:S(2)}) copy-start(f32[8,1,144]{2,1,0:T(1,128)} %param.3) | copy-start | bytes 13828
  92.5 13.6 %all-to-all-start.5 = ((f32[16,8,144]{2,1,0:T(8,128)}), f32[16,8,144]{2,1,0:T(8,128)S(1)}, u32[]{:S(2)}, u32[]{:S(2)}) async-start(f32[16,8,144]{2,1,0:T(8,128)} %convolution_bitcast_fusion), calls=%async_computation.5 | async-start | bytes 262144 | tf_op jit(solution)/shard_map/all_to_all | solution.py:24
where the time goes:
time: 144 us; the launch traced here: 143 us
  blocking collectives  87.2 us (61%)
  matrix products  18.6 us (13%)
  local copies, waits for them, and re-layouts  16.3 us (11%)
  starting transfers between devices  12.3 us (9%)
  waiting for transfers between devices  6.39 us (4%)
  other arithmetic  1.58 us (1%)
    psum x4, blocking collectives, over_axes(): return functools.reduce(lax.psum, axes, value)  35.5 us
    all_to_all x2, blocking collectives, sent_to_all(): lax.all_to_all(jnp.broadcast_to(value[None], (size, *value.shape)), axis,...  26.8 us
    all_to_all x2, blocking collectives, summed_on_arrival(): lax.all_to_all(pieces, axis, split_axis=0, concat_axis=0, tiled=True)  24.9 us
    unnamed x4, local copies, waits for them, and re-layouts  15.2 us
    dot_general x2, matrix products, accumulate(): lax.dot_general(portion, hamiltonian, (((1,), (1,)), ((), ())), preferred...  13 us
    all_to_all x1, starting transfers between devices, summed_on_arrival(): lax.all_to_all(pieces, axis, split_axis=0, concat_axis=0, tiled=True)  7.23 us
    all_to_all x1, waiting for transfers between devices, summed_on_arrival(): lax.all_to_all(pieces, axis, split_axis=0, concat_axis=0, tiled=True)  6.39 us
    dot_general x1, matrix products, accumulate(): return jnp.dot(portion, hamiltonian, preferred_element_type=jnp.float32)  5.55 us
  transfers between devices with their start and end apart: 2, of which 1 were waited for; matrix products, arithmetic and copies ran while one was open for 10% of the time, Pallas kernels for 0%

commit v1 on v0

v1 whole, which is shorter than its diff:
```python
import functools

import jax
import jax.numpy as jnp
from jax import lax
from jax.experimental import pallas as pl
from jax.experimental.pallas import tpu as pltpu
from jax.sharding import PartitionSpec as P

ORDER = 36864
NVEC = 8
GROUP = 16
PIECE = 144
TILE = 256
TILES = 9
BLOCK = TILE * TILES
F32 = jnp.float32
BF16 = jnp.bfloat16


def row_home(tile):
    return jnp.where(tile == TILES - 1, 8, 2 * tile + 1)


def col_home(tile, parity):
    return jnp.where(parity == 0, tile, GROUP - 1 - tile)


def kernel(
    h_ref, v_ref, last_ref, mom_ref,
    h, p0_own, p0, v0_own, v0_in, x0, v1_keep,
    part1, in1, ag1_own, ag1, part2, in2, ag2_own, ag2, part3, in3,
    out_own, out_in, sq, m1_own, m1, m2_own, m2,
    h_sem, p0_s, p0_r, v0_s, v0_r, rs_s, rs_r, ag_s, ag_r, out_s, out_r, m_s, m_r,
):
    row, col = lax.axis_index("row"), lax.axis_index("col")
    parity = lax.rem(row, 2)

    chip = row // 2
    row_red = (parity == 1) | (row == 8)
    row_tile = jnp.where(row == 8, TILES - 1, chip)
    col_slot = jnp.where(parity == 0, col, GROUP - 1 - col)
    col_red = col_slot < TILES
    col_tile = jnp.where(col_red, col_slot, col_slot - 7)

    def peer(axis, index):
        return (index, col) if axis == "row" else (row, index)

    def send(src, dst, s_sem, r_sem, axis, index):
        pltpu.make_async_remote_copy(
            src_ref=src, dst_ref=dst, send_sem=s_sem, recv_sem=r_sem,
            device_id=peer(axis, index), device_id_type=pl.DeviceIdType.MESH,
        ).start()

    def wait_for(ref, sem):
        pltpu.make_async_copy(ref, ref, sem).wait()

    def others(axis):
        me = row if axis == "row" else col
        return [lax.rem(me + k, GROUP) for k in (8, 7, 9, 6, 10, 5, 11, 4, 12, 3, 13, 2, 14, 1, 15)]

    def nth(first, i):
        return lax.rem(first + 1 + i, TILES)

    def h_rows(tile):
        return pl.ds(pl.multiple_of(tile * TILE, TILE), TILE)

    loads = []
    for i in range(TILES):
        rows = h_rows(nth(col_tile, i))
        loads.append(pltpu.make_async_copy(h_ref.at[rows, :], h.at[rows, :], h_sem.at[i]))
        loads[-1].start()

    barrier = pltpu.get_barrier_semaphore()
    for axis in ("row", "col"):
        for index in others(axis):
            pl.semaphore_signal(
                barrier, inc=1, device_id=peer(axis, index), device_id_type=pl.DeviceIdType.MESH
            )

    lane = lax.broadcasted_iota(jnp.int32, (NVEC, TILE), 1)
    start = jnp.concatenate(
        [v_ref[:, 0, :], jnp.zeros((NVEC, TILE - PIECE), F32)], axis=1
    )
    v0_own[...] = start
    p0_own[...] = start.astype(BF16)
    sq[0] = jnp.sum(start * start, axis=1, keepdims=True)
    for n in (1, 2, 3):
        sq[n] = jnp.zeros((NVEC, 1), F32)
    pl.semaphore_wait(barrier, 2 * (GROUP - 1))

    for index in others("row"):
        send(p0_own, p0.at[row], p0_s, p0_r, "row", index)
    p0[row] = start.astype(BF16)

    first_tile = (PIECE * row) // TILE
    last_tile = (PIECE * row + PIECE - 1) // TILE
    for n, tile in enumerate((first_tile, last_tile)):
        home = row_home(tile)
        slot = row - (TILE * tile) // PIECE
        wanted = jnp.bool_(True) if n == 0 else last_tile != first_tile

        @pl.when(wanted & (home != row))
        def _():
            send(v0_own, v0_in.at[slot], v0_s.at[n], v0_r.at[slot], "row", home)

        @pl.when(wanted & (home == row))
        def _():
            v0_in[slot] = start

    wait_for(p0.at[pl.ds(0, GROUP - 1)], p0_r)
    tiles = [jnp.zeros((NVEC, TILE), F32) for _ in range(TILES)]
    for j in range(GROUP):
        at, shift = divmod(PIECE * j, TILE)
        piece = p0[j].astype(F32)
        turned = pltpu.roll(piece, shift, axis=1) if shift else piece
        tiles[at] = jnp.where((lane >= shift) & (lane < shift + PIECE), turned, tiles[at])
        if shift + PIECE > TILE:
            tiles[at + 1] = jnp.where(lane < shift + PIECE - TILE, turned, tiles[at + 1])
    for k in range(TILES):
        x0[k] = tiles[k].astype(BF16)

    def multiply(x, turned, first, is_red, axis, part, arrived, n):
        me = row if axis == "row" else col
        narrow = jnp.concatenate([x[k] for k in range(TILES)], axis=1)
        for i in range(TILES):
            tile = nth(first, i)
            if n == 0:
                loads[i].wait()
            if turned:
                block = h[h_rows(tile), :]
                value = lax.dot_general(
                    narrow, block, (((1,), (1,)), ((), ())), preferred_element_type=F32
                )
            else:
                value = jnp.dot(narrow, h[:, h_rows(tile)], preferred_element_type=F32)
            home = row_home(tile) if axis == "row" else col_home(tile, parity)
            if i < TILES - 1:
                part[i] = value
                send(part.at[i], arrived.at[me], rs_s.at[n], rs_r.at[n], axis, home)
            else:

                @pl.when(is_red)
                def _():
                    arrived[me] = value

                @pl.when(jnp.logical_not(is_red))
                def _():
                    part[i] = value
                    send(part.at[i], arrived.at[me], rs_s.at[n], rs_r.at[n], axis, home)

    def summed(arrived, n):
        wait_for(arrived.at[pl.ds(0, GROUP - 1)], rs_r.at[n])
        terms = [arrived[j] for j in range(GROUP)]
        while len(terms) > 1:
            terms = [terms[k] + terms[k + 1] for k in range(0, len(terms), 2)]
        return terms[0]

    def to_all(value, own, dest, tile, axis, n):
        own[...] = value.astype(BF16)
        for index in others(axis):
            send(own, dest.at[tile], ag_s.at[n], ag_r.at[n], axis, index)
        dest[tile] = value.astype(BF16)

    def gathered(dest, is_red, n):
        @pl.when(is_red)
        def _():
            wait_for(dest.at[pl.ds(0, TILES - 1)], ag_r.at[n])

        @pl.when(jnp.logical_not(is_red))
        def _():
            wait_for(dest, ag_r.at[n])

    def square(value):
        return jnp.sum(value * value, axis=1, keepdims=True)

    multiply(x0, True, col_tile, col_red, "col", part1, in1, 0)

    @pl.when(col_red)
    def _():
        v1 = summed(in1, 0)
        to_all(v1, ag1_own, ag1, col_tile, "col", 0)
        v1_keep[...] = v1
        sq[1] = square(v1)

    gathered(ag1, col_red, 0)

    multiply(ag1, False, row_tile, row_red, "row", part2, in2, 1)

    @pl.when(row_red)
    def _():
        v0 = jnp.zeros((NVEC, TILE), F32)
        for slot in range(3):
            owner = (TILE * row_tile) // PIECE + slot
            offset = PIECE * owner - TILE * row_tile

            @pl.when((offset < TILE) & (owner != row))
            def _():
                wait_for(v0_in.at[slot], v0_r.at[slot])

            turned = pltpu.roll(v0_in[slot], lax.rem(offset + TILE, TILE), axis=1)
            v0 = jnp.where((lane >= offset) & (lane < offset + PIECE), turned, v0)
        v2 = 2.0 * summed(in2, 1) - v0
        to_all(v2, ag2_own, ag2, row_tile, "row", 1)
        sq[2] = square(v2)

    gathered(ag2, row_red, 1)

    multiply(ag2, True, col_tile, col_red, "col", part3, in3, 2)

    def out_dest(slot):
        owner = (TILE * col_tile) // PIECE + slot
        return owner, PIECE * owner < TILE * (col_tile + 1), col_tile - (PIECE * owner) // TILE

    @pl.when(col_red)
    def _():
        v3 = 2.0 * summed(in3, 2) - v1_keep[...]
        out_own[...] = v3
        sq[3] = square(v3)

    wide = lax.broadcasted_iota(jnp.int32, (NVEC, 128), 1)
    sub = lax.broadcasted_iota(jnp.int32, (NVEC, 128), 0)
    packed = jnp.zeros((NVEC, 128), F32)
    for n in range(4):
        packed = jnp.where(wide == 4 * sub + n, sq[n], packed)

    def everywhere(value, own, dest, axis, n):
        me = row if axis == "row" else col
        own[...] = value
        for index in others(axis):
            send(own, dest.at[me], m_s.at[n], m_r.at[n], axis, index)
        dest[me] = value

    def total(dest, n):
        wait_for(dest.at[pl.ds(0, GROUP - 1)], m_r.at[n])
        terms = [dest[j] for j in range(GROUP)]
        while len(terms) > 1:
            terms = [terms[k] + terms[k + 1] for k in range(0, len(terms), 2)]
        return terms[0]

    everywhere(jnp.sum(packed, axis=0, keepdims=True), m1_own, m1, "col", 0)

    for slot in range(3):
        owner, wanted, place = out_dest(slot)

        @pl.when(col_red & wanted & (owner != col))
        def _():
            send(out_own, out_in.at[place], out_s.at[slot], out_r.at[place], "col", owner)

        @pl.when(col_red & wanted & (owner == col))
        def _():
            out_in[place] = out_own[...]

    everywhere(total(m1, 0), m2_own, m2, "row", 1)

    from_tile = (PIECE * col) // TILE
    upto_tile = (PIECE * col + PIECE - 1) // TILE

    @pl.when(col_home(from_tile, parity) != col)
    def _():
        wait_for(out_in.at[0], out_r.at[0])

    @pl.when((upto_tile != from_tile) & (col_home(upto_tile, parity) != col))
    def _():
        wait_for(out_in.at[1], out_r.at[1])

    both = jnp.concatenate([out_in[0], out_in[1]], axis=1)
    begin = PIECE * col - TILE * from_tile
    last_ref[...] = pltpu.roll(both, lax.rem(2 * TILE - begin, 2 * TILE), axis=1)[:, :PIECE]

    wait_for(p0.at[pl.ds(0, GROUP - 1)], p0_s)
    for n, tile in enumerate((first_tile, last_tile)):
        wanted = jnp.bool_(True) if n == 0 else last_tile != first_tile

        @pl.when(wanted & (row_home(tile) != row))
        def _():
            wait_for(v0_own, v0_s.at[n])

    for n, (part, is_red) in enumerate(((part1, col_red), (part2, row_red), (part3, col_red))):

        @pl.when(is_red)
        def _():
            wait_for(part.at[pl.ds(0, TILES - 1)], rs_s.at[n])

        @pl.when(jnp.logical_not(is_red))
        def _():
            wait_for(part, rs_s.at[n])

    for n, is_red in enumerate((col_red, row_red)):

        @pl.when(is_red)
        def _():
            wait_for(p0.at[pl.ds(0, GROUP - 1)], ag_s.at[n])

    for slot in range(3):
        owner, wanted, _place = out_dest(slot)

        @pl.when(col_red & wanted & (owner != col))
        def _():
            wait_for(out_own, out_s.at[slot])

    wait_for(m1.at[pl.ds(0, GROUP - 1)], m_s.at[0])

    squares = total(m2, 1) / ORDER
    spread = jnp.broadcast_to(squares, (NVEC, 128))
    by_order = [
        jnp.sum(jnp.where(wide == 4 * sub + n, spread, 0.0), axis=1, keepdims=True)
        for n in range(4)
    ]
    mom_ref[...] = jnp.concatenate(
        [by_order[0]] + [2.0 * by_order[n] - by_order[0] for n in (1, 2, 3)], axis=1
    )
    wait_for(m2.at[pl.ds(0, GROUP - 1)], m_s.at[1])


def per_device(hamiltonian, start_vectors):
    dma = pltpu.SemaphoreType.DMA
    rowed = pltpu.VMEM((GROUP, 1, 128), F32)
    tile = pltpu.VMEM((NVEC, TILE), F32)
    narrow = pltpu.VMEM((NVEC, TILE), BF16)
    return pl.pallas_call(
        kernel,
        out_shape=(
            jax.ShapeDtypeStruct((NVEC, PIECE), F32),
            jax.ShapeDtypeStruct((NVEC, 4), F32),
        ),
        in_specs=[
            pl.BlockSpec(memory_space=pl.ANY),
            pl.BlockSpec(memory_space=pltpu.VMEM),
        ],
        out_specs=(
            pl.BlockSpec(memory_space=pltpu.VMEM),
            pl.BlockSpec(memory_space=pltpu.VMEM),
        ),
        scratch_shapes=[
            pltpu.VMEM((BLOCK, BLOCK), BF16),
            narrow, pltpu.VMEM((GROUP, NVEC, TILE), BF16),
            tile, pltpu.VMEM((3, NVEC, TILE), F32),
            pltpu.VMEM((TILES, NVEC, TILE), BF16), tile,
            pltpu.VMEM((TILES, NVEC, TILE), F32), pltpu.VMEM((GROUP, NVEC, TILE), F32),
            narrow, pltpu.VMEM((TILES, NVEC, TILE), BF16),
            pltpu.VMEM((TILES, NVEC, TILE), F32), pltpu.VMEM((GROUP, NVEC, TILE), F32),
            narrow, pltpu.VMEM((TILES, NVEC, TILE), BF16),
            pltpu.VMEM((TILES, NVEC, TILE), F32), pltpu.VMEM((GROUP, NVEC, TILE), F32),
            tile, pltpu.VMEM((2, NVEC, TILE), F32),
            pltpu.VMEM((4, NVEC, 1), F32),
            pltpu.VMEM((1, 128), F32), rowed, pltpu.VMEM((1, 128), F32), rowed,
            dma((TILES,)), dma(()), dma(()), dma((2,)), dma((3,)), dma((3,)), dma((3,)),
            dma((2,)), dma((2,)), dma((3,)), dma((2,)), dma((2,)), dma((2,)),
        ],
        compiler_params=pltpu.CompilerParams(
            collective_id=0, has_side_effects=True, vmem_limit_bytes=60 * 1024 * 1024
        ),
    )(hamiltonian, start_vectors)


def solution(mesh):
    return jax.shard_map(
        per_device,
        mesh=mesh,
        in_specs=(P("row", "col"), P(None, "col", "row")),
        out_specs=(P(None, ("row", "col")), P()),
        check_vma=False,
    )
```

time: 144 us -> 64.4 us (0.45)
  the two profiles are of different devices: /device:TPU:2 before, /device:TPU:1 now
where the time goes in v1:
time: 64.4 us; the launch traced here: 64.2 us
  Pallas kernels  60.9 us (95%)
  local copies, waits for them, and re-layouts  2.62 us (4%)
    pallas_call x1, Pallas kernels, per_device(): pl.pallas_call(kernel, out_shape=(jax.ShapeDtypeStruct((NVEC, PIECE), F32...  60.9 us
    pallas_call x1, local copies, waits for them, and re-layouts, per_device(): pl.pallas_call(kernel, out_shape=(jax.ShapeDtypeStruct((NVEC, PIECE), F32...  1.32 us
    unnamed x1, local copies, waits for them, and re-layouts  1.29 us

profile of v1, /device:TPU:1, one launch (start us, length us, event | category | flops | bytes accessed | tf_op | source)
XLA Modules:
  0.0 64.2 jit_solution(11831924931201581309)
XLA Ops:
  0.6 60.9 %shard_map.41 = (f32[8,144]{1,0:T(8,128)}, f32[8,4]{1,0:T(8,128)}) custom-call(bf16[2304,2304]{1,0:T(8,128)(2,1)} %h_ref.1, f32[8,1,144]{2,1,0:T(1,128)} %v_ref.1), custom_call_target="tpu_custom_call" | custom-call | tf_op jit(solution)/shard_map/pallas_call | solution.py:321
  61.6 1.3 %copy.4 = f32[8,4]{0,1:T(4,128)} copy(f32[8,4]{1,0:T(8,128)} %get-tuple-element.3) | data formatting | bytes 256 | tf_op jit(solution)/shard_map/pallas_call | solution.py:321
  62.9 1.3 %copy.6 = f32[8,144]{1,0:T(8,128)} copy(f32[8,144]{1,0:T(8,128)} %get-tuple-element.6) | data formatting | bytes 9216

commit v2 on v1

v2 whole, which is shorter than its diff:
```python
import functools

import jax
import jax.numpy as jnp
from jax import lax
from jax.experimental import pallas as pl
from jax.experimental.pallas import tpu as pltpu
from jax.sharding import PartitionSpec as P

ORDER = 36864
NVEC = 8
GROUP = 16
PIECE = 144
TILE = 256
TILES = 9
BLOCK = TILE * TILES
F32 = jnp.float32
BF16 = jnp.bfloat16


def row_home(tile):
    return jnp.where(tile == TILES - 1, 8, 2 * tile + 1)


def col_home(tile, parity):
    return jnp.where(parity == 0, tile, GROUP - 1 - tile)


def kernel(
    h_ref, v_ref, last_ref, mom_ref,
    v_own, h, h_t, p0_own, p0, v0_own, v0_in, x0, v1_keep,
    part1, in1, ag1_own, ag1, part2, in2, ag2_own, ag2, part3, in3,
    out_own, out_in, sq, m1_own, m1, m2_own, m2,
    v_sem, h_sem, p0_s, p0_r, v0_s, v0_r, rs_s, rs_r, ag_s, ag_r, out_s, out_r, m_s, m_r,
):
    row, col = lax.axis_index("row"), lax.axis_index("col")
    parity = lax.rem(row, 2)

    chip = row // 2
    row_red = (parity == 1) | (row == 8)
    row_tile = jnp.where(row == 8, TILES - 1, chip)
    col_tiles = (col, GROUP - 1 - col)
    col_reds = tuple((parity == 1) & (tile < TILES) for tile in col_tiles)
    col_red = col_reds[1]
    col_slot = jnp.where(parity == 0, col, GROUP - 1 - col)
    col_tile = jnp.where(col_slot < TILES, col_slot, col_slot - 7)
    odd_row = row + 1 - parity
    mate_row = row + 1 - 2 * parity

    def peer(axis, index):
        return (index, col) if axis == "row" else (row, index)

    def send_to(src, dst, s_sem, r_sem, device):
        pltpu.make_async_remote_copy(
            src_ref=src, dst_ref=dst, send_sem=s_sem, recv_sem=r_sem,
            device_id=device, device_id_type=pl.DeviceIdType.MESH,
        ).start()

    def send(src, dst, s_sem, r_sem, axis, index):
        send_to(src, dst, s_sem, r_sem, peer(axis, index))

    def wait_for(ref, sem):
        pltpu.make_async_copy(ref, ref, sem).wait()

    def others(axis):
        me = row if axis == "row" else col
        return [lax.rem(me + k, GROUP) for k in (8, 7, 9, 6, 10, 5, 11, 4, 12, 3, 13, 2, 14, 1, 15)]

    def nth(first, i):
        return lax.rem(first + 1 + i, TILES)

    def span(tile):
        return pl.ds(pl.multiple_of(tile * TILE, TILE), TILE)

    def load(i):
        return pltpu.make_async_copy(h_ref.at[span(i), :], h.at[span(i), :], h_sem.at[i])

    barrier = pltpu.get_barrier_semaphore()
    for axis in ("row", "col"):
        for index in others(axis):
            pl.semaphore_signal(
                barrier, inc=1, device_id=peer(axis, index), device_id_type=pl.DeviceIdType.MESH
            )
    for index in others("col"):
        pl.semaphore_signal(
            barrier, inc=1, device_id=(mate_row, index), device_id_type=pl.DeviceIdType.MESH
        )

    fetch = pltpu.make_async_copy(v_ref, v_own, v_sem)
    fetch.start()
    for i in range(TILES):
        load(i).start()

    lane = lax.broadcasted_iota(jnp.int32, (NVEC, TILE), 1)
    fetch.wait()
    start = jnp.concatenate(
        [v_own[:, 0, :], jnp.zeros((NVEC, TILE - PIECE), F32)], axis=1
    )
    v0_own[...] = start
    p0_own[...] = start.astype(BF16)
    sq[0] = jnp.sum(start * start, axis=1, keepdims=True)
    for n in (1, 2, 3):
        sq[n] = jnp.zeros((NVEC, 1), F32)
    pl.semaphore_wait(barrier, 3 * (GROUP - 1))

    for index in others("row"):
        send(p0_own, p0.at[row], p0_s, p0_r, "row", index)
    p0[row] = start.astype(BF16)

    first_tile = (PIECE * row) // TILE
    last_tile = (PIECE * row + PIECE - 1) // TILE
    for n, tile in enumerate((first_tile, last_tile)):
        home = row_home(tile)
        slot = row - (TILE * tile) // PIECE
        wanted = jnp.bool_(True) if n == 0 else last_tile != first_tile

        @pl.when(wanted & (home != row))
        def _():
            send(v0_own, v0_in.at[slot], v0_s.at[n], v0_r.at[slot], "row", home)

        @pl.when(wanted & (home == row))
        def _():
            v0_in[slot] = start

    @pl.loop(0, TILES)
    def _(i):
        load(i).wait()
        for k in range(TILES):
            h_t[k * TILE : (k + 1) * TILE, span(i)] = h[span(i), k * TILE : (k + 1) * TILE].T

    wait_for(p0.at[pl.ds(0, GROUP - 1)], p0_r)
    tiles = [jnp.zeros((NVEC, TILE), F32) for _ in range(TILES)]
    for j in range(GROUP):
        at, shift = divmod(PIECE * j, TILE)
        piece = p0[j].astype(F32)
        turned = pltpu.roll(piece, shift, axis=1) if shift else piece
        tiles[at] = jnp.where((lane >= shift) & (lane < shift + PIECE), turned, tiles[at])
        if shift + PIECE > TILE:
            tiles[at + 1] = jnp.where(lane < shift + PIECE - TILE, turned, tiles[at + 1])
    for k in range(TILES):
        x0[k] = tiles[k].astype(BF16)

    def multiply(x, matrix, first, is_red, axis, part, arrived, n):
        narrow = jnp.concatenate([x[k] for k in range(TILES)], axis=1)

        def hand_over(i, value):
            tile = nth(first, i)
            part[i] = value
            if axis == "row":
                device, place, arrival = (row_home(tile), col), arrived.at[row], rs_r.at[n, 0]
            else:
                device = (odd_row, col_home(tile, parity))
                place, arrival = arrived.at[parity, col], rs_r.at[n, parity]
            send_to(part.at[i], place, rs_s.at[n], arrival, device)

        before = None
        for i in range(TILES):
            value = jnp.dot(
                narrow, matrix[:, span(nth(first, i))], preferred_element_type=F32
            )
            if i:
                hand_over(i - 1, before)
            before = value

        @pl.when(is_red)
        def _():
            if axis == "row":
                arrived[row] = before
            else:
                arrived[1, col] = before

        @pl.when(jnp.logical_not(is_red))
        def _():
            hand_over(TILES - 1, before)

    def summed(arrived, n, group, count):
        wait_for(arrived.at[pl.ds(0, count)], rs_r.at[n, group])
        terms = [arrived[j] for j in range(GROUP)]
        while len(terms) > 1:
            terms = [terms[k] + terms[k + 1] for k in range(0, len(terms), 2)]
        return terms[0]

    def to_all(value, own, dest, tile, s_sem, r_sem, devices, mine):
        own[...] = value.astype(BF16)
        for device in devices:
            send_to(own, dest.at[tile], s_sem, r_sem, device)
        if mine:
            dest[tile] = value.astype(BF16)

    def gathered(dest, is_red, n):
        @pl.when(is_red)
        def _():
            wait_for(dest.at[pl.ds(0, TILES - 1)], ag_r.at[n])

        @pl.when(jnp.logical_not(is_red))
        def _():
            wait_for(dest, ag_r.at[n])

    def square(value):
        return jnp.sum(value * value, axis=1, keepdims=True)

    multiply(x0, h_t, col_tile, col_red, "col", part1, in1, 0)

    for group in (0, 1):

        @pl.when(col_reds[group])
        def _():
            v1 = summed(in1.at[group], 0, group, GROUP - group)
            devices = [(row - 1 + group, index) for index in others("col")]
            if group == 0:
                devices.append((row - 1, col))
            to_all(
                v1, ag1_own.at[group], ag1, col_tiles[group],
                ag_s.at[group], ag_r.at[0], devices, group == 1,
            )
            v1_keep[group] = v1
            sq[1] += square(v1)

    gathered(ag1, col_red, 0)

    multiply(ag1, h, row_tile, row_red, "row", part2, in2, 1)

    @pl.when(row_red)
    def _():
        v0 = jnp.zeros((NVEC, TILE), F32)
        for slot in range(3):
            owner = (TILE * row_tile) // PIECE + slot
            offset = PIECE * owner - TILE * row_tile

            @pl.when((offset < TILE) & (owner != row))
            def _():
                wait_for(v0_in.at[slot], v0_r.at[slot])

            turned = pltpu.roll(v0_in[slot], lax.rem(offset + TILE, TILE), axis=1)
            v0 = jnp.where((lane >= offset) & (lane < offset + PIECE), turned, v0)
        v2 = 2.0 * summed(in2, 1, 0, GROUP - 1) - v0
        devices = [(index, col) for index in others("row")]
        to_all(v2, ag2_own, ag2, row_tile, ag_s.at[2], ag_r.at[1], devices, True)
        sq[2] = square(v2)

    gathered(ag2, row_red, 1)

    multiply(ag2, h_t, col_tile, col_red, "col", part3, in3, 2)

    def out_dest(group, slot):
        tile = col_tiles[group]
        owner = (TILE * tile) // PIECE + slot
        wanted = col_reds[group] & (PIECE * owner < TILE * (tile + 1))
        return owner, wanted, tile - (PIECE * owner) // TILE

    for group in (0, 1):

        @pl.when(col_reds[group])
        def _():
            v3 = 2.0 * summed(in3.at[group], 2, group, GROUP - group) - v1_keep[group]
            out_own[group] = v3
            sq[3] += square(v3)

    wide = lax.broadcasted_iota(jnp.int32, (NVEC, 128), 1)
    sub = lax.broadcasted_iota(jnp.int32, (NVEC, 128), 0)
    packed = jnp.zeros((NVEC, 128), F32)
    for n in range(4):
        packed = jnp.where(wide == 4 * sub + n, sq[n], packed)

    def everywhere(value, own, dest, axis, n):
        me = row if axis == "row" else col
        own[...] = value
        for index in others(axis):
            send(own, dest.at[me], m_s.at[n], m_r.at[n], axis, index)
        dest[me] = value

    def total(dest, n):
        wait_for(dest.at[pl.ds(0, GROUP - 1)], m_r.at[n])
        terms = [dest[j] for j in range(GROUP)]
        while len(terms) > 1:
            terms = [terms[k] + terms[k + 1] for k in range(0, len(terms), 2)]
        return terms[0]

    everywhere(jnp.sum(packed, axis=0, keepdims=True), m1_own, m1, "col", 0)

    for group in (0, 1):
        for slot in range(3):
            owner, wanted, place = out_dest(group, slot)
            mine = (owner == col) if group else jnp.bool_(False)

            @pl.when(wanted & jnp.logical_not(mine))
            def _():
                send_to(
                    out_own.at[group], out_in.at[place], out_s.at[group, slot], out_r.at[place],
                    (row - 1 + group, owner),
                )

            if group:

                @pl.when(wanted & mine)
                def _():
                    out_in[place] = out_own[group]

    everywhere(total(m1, 0), m2_own, m2, "row", 1)

    from_tile = (PIECE * col) // TILE
    upto_tile = (PIECE * col + PIECE - 1) // TILE

    def elsewhere(tile):
        return (parity == 0) | (col_home(tile, parity) != col)

    @pl.when(elsewhere(from_tile))
    def _():
        wait_for(out_in.at[0], out_r.at[0])

    @pl.when((upto_tile != from_tile) & elsewhere(upto_tile))
    def _():
        wait_for(out_in.at[1], out_r.at[1])

    both = jnp.concatenate([out_in[0], out_in[1]], axis=1)
    begin = PIECE * col - TILE * from_tile
    last_ref[...] = pltpu.roll(both, lax.rem(2 * TILE - begin, 2 * TILE), axis=1)[:, :PIECE]

    wait_for(p0.at[pl.ds(0, GROUP - 1)], p0_s)
    for n, tile in enumerate((first_tile, last_tile)):
        wanted = jnp.bool_(True) if n == 0 else last_tile != first_tile

        @pl.when(wanted & (row_home(tile) != row))
        def _():
            wait_for(v0_own, v0_s.at[n])

    for n, (part, is_red) in enumerate(((part1, col_red), (part2, row_red), (part3, col_red))):

        @pl.when(is_red)
        def _():
            wait_for(part.at[pl.ds(0, TILES - 1)], rs_s.at[n])

        @pl.when(jnp.logical_not(is_red))
        def _():
            wait_for(part, rs_s.at[n])

    for n, is_red in enumerate((*col_reds, row_red)):

        @pl.when(is_red)
        def _():
            wait_for(p0.at[pl.ds(0, GROUP if n == 0 else GROUP - 1)], ag_s.at[n])

    for group in (0, 1):
        for slot in range(3):
            owner, wanted, _place = out_dest(group, slot)
            mine = (owner == col) if group else jnp.bool_(False)

            @pl.when(wanted & jnp.logical_not(mine))
            def _():
                wait_for(out_own.at[group], out_s.at[group, slot])

    wait_for(m1.at[pl.ds(0, GROUP - 1)], m_s.at[0])

    squares = total(m2, 1) / ORDER
    spread = jnp.broadcast_to(squares, (NVEC, 128))
    by_order = [
        jnp.sum(jnp.where(wide == 4 * sub + n, spread, 0.0), axis=1, keepdims=True)
        for n in range(4)
    ]
    mom_ref[...] = jnp.concatenate(
        [by_order[0]] + [2.0 * by_order[n] - by_order[0] for n in (1, 2, 3)], axis=1
    )
    wait_for(m2.at[pl.ds(0, GROUP - 1)], m_s.at[1])


def per_device(hamiltonian, start_vectors):
    dma = pltpu.SemaphoreType.DMA
    rowed = pltpu.VMEM((GROUP, 1, 128), F32)
    tile = pltpu.VMEM((NVEC, TILE), F32)
    narrow = pltpu.VMEM((NVEC, TILE), BF16)
    return pl.pallas_call(
        kernel,
        out_shape=(
            pltpu.VMEM((NVEC, PIECE), F32),
            pltpu.VMEM((NVEC, 4), F32),
        ),
        in_specs=[
            pl.BlockSpec(memory_space=pl.ANY),
            pl.BlockSpec(memory_space=pl.ANY),
        ],
        out_specs=(
            pl.BlockSpec(memory_space=pltpu.VMEM),
            pl.BlockSpec(memory_space=pltpu.VMEM),
        ),
        scratch_shapes=[
            pltpu.VMEM((NVEC, 1, PIECE), F32),
            pltpu.VMEM((BLOCK, BLOCK), BF16),
            pltpu.VMEM((BLOCK, BLOCK), BF16),
            narrow, pltpu.VMEM((GROUP, NVEC, TILE), BF16),
            tile, pltpu.VMEM((3, NVEC, TILE), F32),
            pltpu.VMEM((TILES, NVEC, TILE), BF16), pltpu.VMEM((2, NVEC, TILE), F32),
            pltpu.VMEM((TILES, NVEC, TILE), F32), pltpu.VMEM((2, GROUP, NVEC, TILE), F32),
            pltpu.VMEM((2, NVEC, TILE), BF16), pltpu.VMEM((TILES, NVEC, TILE), BF16),
            pltpu.VMEM((TILES, NVEC, TILE), F32), pltpu.VMEM((GROUP, NVEC, TILE), F32),
            narrow, pltpu.VMEM((TILES, NVEC, TILE), BF16),
            pltpu.VMEM((TILES, NVEC, TILE), F32), pltpu.VMEM((2, GROUP, NVEC, TILE), F32),
            pltpu.VMEM((2, NVEC, TILE), F32), pltpu.VMEM((2, NVEC, TILE), F32),
            pltpu.VMEM((4, NVEC, 1), F32),
            pltpu.VMEM((1, 128), F32), rowed, pltpu.VMEM((1, 128), F32), rowed,
            dma(()), dma((TILES,)), dma(()), dma(()), dma((2,)), dma((3,)), dma((3,)),
            dma((3, 2)), dma((3,)), dma((2,)), dma((2, 3)), dma((2,)), dma((2,)), dma((2,)),
        ],
        compiler_params=pltpu.CompilerParams(
            collective_id=0, has_side_effects=True, vmem_limit_bytes=60 * 1024 * 1024
        ),
    )(hamiltonian, start_vectors)


def solution(mesh):
    return jax.shard_map(
        per_device,
        mesh=mesh,
        in_specs=(P("row", "col"), P(None, "col", "row")),
        out_specs=(P(None, ("row", "col")), P()),
        check_vma=False,
    )
```

time: 64.4 us -> 51.1 us (0.79)
  Pallas kernels: 60.9 us -> 49.1 us
  local copies, waits for them, and re-layouts: 2.62 us -> 1.25 us
    pallas_call x1, Pallas kernels: 60.9 us -> 49.1 us  [per_device(): pl.pallas_call(kernel, out_shape=(pltpu.VMEM((NVEC, PIECE), F32), pltpu.V...]
    unnamed x1, local copies, waits for them, and re-layouts: 1.29 us -> 0.6 us
    pallas_call x1, local copies, waits for them, and re-layouts: 1.32 us -> 0.65 us  [per_device(): pl.pallas_call(kernel, out_shape=(pltpu.VMEM((NVEC, PIECE), F32), pltpu.V...]
where the time goes in v2:
time: 51.1 us; the launch traced here: 51 us
  Pallas kernels  49.1 us (96%)
  local copies, waits for them, and re-layouts  1.25 us (2%)
  between operations  0.64 us (1%)
    pallas_call x1, Pallas kernels, per_device(): pl.pallas_call(kernel, out_shape=(pltpu.VMEM((NVEC, PIECE), F32), pltpu.V...  49.1 us

profile of v2, /device:TPU:1, one launch (start us, length us, event | category | flops | bytes accessed | tf_op | source)
XLA Modules:
  0.0 51.0 jit_solution(9674471236078498536)
XLA Ops:
  0.6 49.1 %shard_map.41 = (f32[8,144]{1,0:T(8,128)S(1)}, f32[8,4]{1,0:T(8,128)S(1)}) custom-call(bf16[2304,2304]{1,0:T(8,128)(2,1)} %h_ref.1, f32[8,1,144]{2,1,0:T(1,128)} %v_ref.1), custom_call_target="tpu_custom_call" | custom-call | tf_op jit(solution)/shard_map/pallas_call | solution.py:371
  49.8 0.6 %copy.6 = f32[8,144]{1,0:T(8,128)} copy(f32[8,144]{1,0:T(8,128)S(1)} %get-tuple-element.4) | data formatting | bytes 9216
  50.4 0.7 %copy.4 = f32[8,4]{0,1:T(4,128)} copy(f32[8,4]{1,0:T(8,128)S(1)} %get-tuple-element.3) | data formatting | bytes 256 | tf_op jit(solution)/shard_map/pallas_call | solution.py:371

commit v3 on v2

--- a/solution.py
+++ b/solution.py
@@ -30,7 +30,7 @@
     h_ref, v_ref, last_ref, mom_ref,
     v_own, h, h_t, p0_own, p0, v0_own, v0_in, x0, v1_keep,
     part1, in1, ag1_own, ag1, part2, in2, ag2_own, ag2, part3, in3,
-    out_own, out_in, sq, m1_own, m1, m2_own, m2,
+    sofar, out_own, out_in, sq, m1_own, m1, m2_own, m2,
     v_sem, h_sem, p0_s, p0_r, v0_s, v0_r, rs_s, rs_r, ag_s, ag_r, out_s, out_r, m_s, m_r,
 ):
     row, col = lax.axis_index("row"), lax.axis_index("col")
@@ -63,8 +63,13 @@
         pltpu.make_async_copy(ref, ref, sem).wait()
 
     def others(axis):
-        me = row if axis == "row" else col
-        return [lax.rem(me + k, GROUP) for k in (8, 7, 9, 6, 10, 5, 11, 4, 12, 3, 13, 2, 14, 1, 15)]
+        if axis == "row":
+            return [lax.rem(row + k, GROUP) for k in (8, 7, 9, 6, 10, 5, 11, 4, 12, 3, 13, 2, 14, 1, 15)]
+        steps = [(dx, dy) for dx in range(4) for dy in range(4) if dx or dy]
+        steps.sort(key=lambda s: -min(s[0], 4 - s[0]) - min(s[1], 4 - s[1]))
+        return [
+            lax.rem(col // 4 + dx, 4) * 4 + lax.rem(lax.rem(col, 4) + dy, 4) for dx, dy in steps
+        ]
 
     def nth(first, i):
         return lax.rem(first + 1 + i, TILES)
@@ -107,21 +112,6 @@
         send(p0_own, p0.at[row], p0_s, p0_r, "row", index)
     p0[row] = start.astype(BF16)
 
-    first_tile = (PIECE * row) // TILE
-    last_tile = (PIECE * row + PIECE - 1) // TILE
-    for n, tile in enumerate((first_tile, last_tile)):
-        home = row_home(tile)
-        slot = row - (TILE * tile) // PIECE
-        wanted = jnp.bool_(True) if n == 0 else last_tile != first_tile
-
-        @pl.when(wanted & (home != row))
-        def _():
-            send(v0_own, v0_in.at[slot], v0_s.at[n], v0_r.at[slot], "row", home)
-
-        @pl.when(wanted & (home == row))
-        def _():
-            v0_in[slot] = start
-
     @pl.loop(0, TILES)
     def _(i):
         load(i).wait()
@@ -140,8 +130,20 @@
     for k in range(TILES):
         x0[k] = tiles[k].astype(BF16)
 
-    def multiply(x, matrix, first, is_red, axis, part, arrived, n):
-        narrow = jnp.concatenate([x[k] for k in range(TILES)], axis=1)
+    def multiply(x, matrix, first, is_red, axis, part, arrived, n, arrive, early, late):
+        def product(tiles, columns):
+            return sum(
+                jnp.dot(x[k], matrix[span(k), columns], preferred_element_type=F32)
+                for k in tiles
+            )
+
+        if early:
+            for k in early:
+                arrive(k)
+            for i in range(TILES):
+                sofar[i] = product(early, slice(i * TILE, (i + 1) * TILE))
+            for k in late:
+                arrive(k)
 
         def hand_over(i, value):
             tile = nth(first, i)
@@ -155,9 +157,10 @@
 
         before = None
         for i in range(TILES):
-            value = jnp.dot(
-                narrow, matrix[:, span(nth(first, i))], preferred_element_type=F32
-            )
+            tile = nth(first, i)
+            value = product(late, span(tile))
+            if early:
+                value = value + sofar[tile]
             if i:
                 hand_over(i - 1, before)
             before = value
@@ -187,19 +190,33 @@
         if mine:
             dest[tile] = value.astype(BF16)
 
-    def gathered(dest, is_red, n):
-        @pl.when(is_red)
-        def _():
-            wait_for(dest.at[pl.ds(0, TILES - 1)], ag_r.at[n])
-
-        @pl.when(jnp.logical_not(is_red))
-        def _():
-            wait_for(dest, ag_r.at[n])
+    def gathered(dest, is_red, own, n):
+        def arrive(tile):
+            @pl.when(jnp.logical_not(is_red & (own == tile)))
+            def _():
+                wait_for(dest.at[tile], ag_r.at[n, tile])
+
+        return arrive
 
     def square(value):
         return jnp.sum(value * value, axis=1, keepdims=True)
 
-    multiply(x0, h_t, col_tile, col_red, "col", part1, in1, 0)
+    multiply(x0, h_t, col_tile, col_red, "col", part1, in1, 0, None, (), tuple(range(TILES)))
+
+    first_tile = (PIECE * row) // TILE
+    last_tile = (PIECE * row + PIECE - 1) // TILE
+    for n, tile in enumerate((first_tile, last_tile)):
+        home = row_home(tile)
+        slot = row - (TILE * tile) // PIECE
+        wanted = jnp.bool_(True) if n == 0 else last_tile != first_tile
+
+        @pl.when(wanted & (home != row))
+        def _():
+            send(v0_own, v0_in.at[slot], v0_s.at[n], v0_r.at[slot], "row", home)
+
+        @pl.when(wanted & (home == row))
+        def _():
+            v0_in[slot] = start
 
     for group in (0, 1):
 
@@ -211,14 +228,18 @@
                 devices.append((row - 1, col))
             to_all(
                 v1, ag1_own.at[group], ag1, col_tiles[group],
-                ag_s.at[group], ag_r.at[0], devices, group == 1,
+                ag_s.at[group], ag_r.at[0, col_tiles[group]], devices, group == 1,
             )
             v1_keep[group] = v1
             sq[1] += square(v1)
 
-    gathered(ag1, col_red, 0)
-
-    multiply(ag1, h, row_tile, row_red, "row", part2, in2, 1)
+    across = jnp.where(parity == 0, col // 4, 3 - col // 4)
+    base = jnp.where((across == 1) | (across == 2), 4, 0)
+    near = [base + k for k in range(4)]
+    far = [4 - base + k for k in range(4)] + [8]
+    arrive = gathered(ag1, col_red, col_tiles[1], 0)
+
+    multiply(ag1, h, row_tile, row_red, "row", part2, in2, 1, arrive, near, far)
 
     @pl.when(row_red)
     def _():
@@ -235,12 +256,14 @@
             v0 = jnp.where((lane >= offset) & (lane < offset + PIECE), turned, v0)
         v2 = 2.0 * summed(in2, 1, 0, GROUP - 1) - v0
         devices = [(index, col) for index in others("row")]
-        to_all(v2, ag2_own, ag2, row_tile, ag_s.at[2], ag_r.at[1], devices, True)
+        to_all(v2, ag2_own, ag2, row_tile, ag_s.at[2], ag_r.at[1, row_tile], devices, True)
         sq[2] = square(v2)
 
-    gathered(ag2, row_red, 1)
-
-    multiply(ag2, h_t, col_tile, col_red, "col", part3, in3, 2)
+    near = [lax.rem(chip + k, 8) for k in (0, 1, 7, 2, 6)]
+    far = [lax.rem(chip + k, 8) for k in (3, 5, 4)] + [8]
+    arrive = gathered(ag2, row_red, row_tile, 1)
+
+    multiply(ag2, h_t, col_tile, col_red, "col", part3, in3, 2, arrive, near, far)
 
     def out_dest(group, slot):
         tile = col_tiles[group]
@@ -394,11 +417,12 @@
             pltpu.VMEM((TILES, NVEC, TILE), F32), pltpu.VMEM((GROUP, NVEC, TILE), F32),
             narrow, pltpu.VMEM((TILES, NVEC, TILE), BF16),
             pltpu.VMEM((TILES, NVEC, TILE), F32), pltpu.VMEM((2, GROUP, NVEC, TILE), F32),
+            pltpu.VMEM((TILES, NVEC, TILE), F32),
             pltpu.VMEM((2, NVEC, TILE), F32), pltpu.VMEM((2, NVEC, TILE), F32),
             pltpu.VMEM((4, NVEC, 1), F32),
             pltpu.VMEM((1, 128), F32), rowed, pltpu.VMEM((1, 128), F32), rowed,
             dma(()), dma((TILES,)), dma(()), dma(()), dma((2,)), dma((3,)), dma((3,)),
-            dma((3, 2)), dma((3,)), dma((2,)), dma((2, 3)), dma((2,)), dma((2,)), dma((2,)),
+            dma((3, 2)), dma((3,)), dma((2, TILES)), dma((2, 3)), dma((2,)), dma((2,)), dma((2,)),
         ],
         compiler_params=pltpu.CompilerParams(
             collective_id=0, has_side_effects=True, vmem_limit_bytes=60 * 1024 * 1024

time: 51.1 us -> 50.2 us (0.982)
  Pallas kernels: 49.1 us -> 48.2 us
    pallas_call x1, Pallas kernels: 49.1 us -> 48.2 us  [per_device(): pl.pallas_call(kernel, out_shape=(pltpu.VMEM((NVEC, PIECE), F32), pltpu.V...]
where the time goes in v3:
time: 50.2 us; the launch traced here: 50.1 us
  Pallas kernels  48.2 us (96%)
  local copies, waits for them, and re-layouts  1.25 us (2%)
  between operations  0.64 us (1%)
    pallas_call x1, Pallas kernels, per_device(): pl.pallas_call(kernel, out_shape=(pltpu.VMEM((NVEC, PIECE), F32), pltpu.V...  48.2 us

profile of v3, /device:TPU:1, one launch (start us, length us, event | category | flops | bytes accessed | tf_op | source)
XLA Modules:
  0.0 50.1 jit_solution(15588544102760187533)
XLA Ops:
  0.6 48.2 %shard_map.41 = (f32[8,144]{1,0:T(8,128)S(1)}, f32[8,4]{1,0:T(8,128)S(1)}) custom-call(bf16[2304,2304]{1,0:T(8,128)(2,1)} %h_ref.1, f32[8,1,144]{2,1,0:T(1,128)} %v_ref.1), custom_call_target="tpu_custom_call" | custom-call | tf_op jit(solution)/shard_map/pallas_call | solution.py:394
  48.8 0.6 %copy.6 = f32[8,144]{1,0:T(8,128)} copy(f32[8,144]{1,0:T(8,128)S(1)} %get-tuple-element.4) | data formatting | bytes 9216
  49.4 0.7 %copy.4 = f32[8,4]{0,1:T(4,128)} copy(f32[8,4]{1,0:T(8,128)S(1)} %get-tuple-element.3) | data formatting | bytes 256 | tf_op jit(solution)/shard_map/pallas_call | solution.py:394
